TPU v7x, 32 devices: a 4x4x1 block of a 4x4x8 slice. The times are simulated.
32 devices in a mesh: batch: 1 (over z), dap: 32 (over y, x, core).
Axes of the slice: x: 4, y: 4, z: 1, core: 2. Of those that a mesh axis runs over, the one named last changes fastest.
The devices are a block of a 4x4x8 slice.
Arguments:
- pair: bfloat16 [512, 512, 128], P(('batch', 'dap'))
- pair_mask: int32 [512, 512], P(('batch', 'dap'))
- ln_in: bfloat16 [2, 2, 128], replicated
- w_proj: bfloat16 [2, 128, 512], replicated
- b_proj: bfloat16 [2, 512], replicated
- w_gate: bfloat16 [2, 128, 128], replicated
- b_gate: bfloat16 [2, 128], replicated
- ln_out: bfloat16 [2, 2, 128], replicated
- w_out: bfloat16 [2, 128, 128], replicated
- b_out: bfloat16 [2, 128], replicated
Outputs:
- output: bfloat16 [512, 512, 128], P(('batch', 'dap'))
All inputs are finite; a program needn't handle non-finite values.
Results may differ from a plain program's by a relative error of at most 0.00381369.
Values are sent between devices in bfloat16 or wider.
A program may use at most 768 MiB of HBM per device.

v0:
```python
import jax
import jax.numpy as jnp
from jax import lax
from jax.sharding import PartitionSpec as P, NamedSharding

LN_EPS = 1e-5


def norm_last(values, scale, offset):
    centred = values - jnp.mean(values, axis=-1, keepdims=True)
    variance = jnp.mean(centred * centred, axis=-1, keepdims=True)
    return centred * lax.rsqrt(variance + LN_EPS) * scale.astype(jnp.float32) + offset.astype(jnp.float32)


def norm_channels(values, scale, offset):
    centred = values - jnp.mean(values, axis=-3, keepdims=True)
    variance = jnp.mean(centred * centred, axis=-3, keepdims=True)
    return (centred * lax.rsqrt(variance + LN_EPS) * scale.astype(jnp.float32)[:, None, None]
            + offset.astype(jnp.float32)[:, None, None])


def gated_side(projected, keep_mask, channels):
    return (keep_mask * jax.nn.sigmoid(projected[channels:2 * channels]) * projected[:channels]).astype(jnp.bfloat16)


def normalize_project(pair, keep_mask, ln_in, w_proj, b_proj, channels):
    normed = norm_last(pair.astype(jnp.float32), ln_in[0], ln_in[1]).astype(jnp.bfloat16)
    projected = jnp.einsum("zc,ijz->cij", w_proj, normed, preferred_element_type=jnp.float32)
    projected = projected + b_proj.astype(jnp.float32)[:, None, None]
    left = gated_side(projected[:2 * channels], keep_mask, channels)
    right = gated_side(projected[2 * channels:], keep_mask, channels)
    return normed, left, right


def finish_layer(pair, normed, tri_sum, w_gate, b_gate, ln_out, w_out, b_out):
    tri_norm = norm_channels(tri_sum, ln_out[0], ln_out[1]).astype(jnp.bfloat16)
    update = jnp.einsum("cij,cz->ijz", tri_norm, w_out, preferred_element_type=jnp.float32) + b_out.astype(jnp.float32)
    gates = jax.nn.sigmoid(jnp.einsum("ijz,zy->ijy", normed, w_gate, preferred_element_type=jnp.float32) + b_gate.astype(jnp.float32))
    return (pair.astype(jnp.float32) + gates * update).astype(jnp.bfloat16)


def solution(mesh):
    row_spec = P(("batch", "dap"), None, None)
    mask_spec = P(("batch", "dap"), None)

    def local_layers(pair, pair_mask, ln_in, w_proj, b_proj, w_gate, b_gate, ln_out, w_out, b_out):
        channels = w_out.shape[1]
        keep_mask = pair_mask.astype(jnp.float32)[None]
        normed, left, right = normalize_project(pair, keep_mask, ln_in[0], w_proj[0], b_proj[0], channels)
        right_all = lax.all_gather(right, "dap", axis=1, tiled=True)
        tri_sum = jnp.einsum("cik,cjk->cij", left, right_all, preferred_element_type=jnp.float32)
        first = finish_layer(pair, normed, tri_sum, w_gate[0], b_gate[0], ln_out[0], w_out[0], b_out[0])
        normed, left, right = normalize_project(first, keep_mask, ln_in[1], w_proj[1], b_proj[1], channels)
        left_cols = lax.all_to_all(left, "dap", 2, 1, tiled=True)
        right_all = lax.all_gather(right, "dap", axis=1, tiled=True)
        tri_sum = jnp.einsum("cki,ckj->cij", left_cols, right_all, preferred_element_type=jnp.float32)
        return finish_layer(first, normed, tri_sum, w_gate[1], b_gate[1], ln_out[1], w_out[1], b_out[1])

    return jax.shard_map(local_layers, mesh=mesh,
                         in_specs=(row_spec, mask_spec, P(), P(), P(), P(), P(), P(), P(), P()),
                         out_specs=row_spec, check_vma=False)
```

profile of v0, /device:TPU:97, one launch (start us, length us, event | category | flops | bytes accessed | tf_op | source)
XLA Modules:
  0.0 590.9 jit_solution(3663052194579590965)
XLA Ops:
  6.6 2.9 copy.63
  10.6 2.6 add_bitcast_fusion.1
  13.2 3.9 fusion.28
  17.1 3.9 copy.67
  21.3 4.5 copy.68
  25.9 3.0 fusion.45
  28.9 192.5 %all-gather.3.cloned.1.call-done = bf16[128,512,512]{2,0,1:T(8,128)(2,1)} async-done(((bf16[128,16,512]{2,0,1:T(8,128)(2,1)}), bf16[128,512,512]{2,0,1:T(8,128)(2,1)}) %all-gather.3.cloned.1.call-update) | async-done | bytes 67108880 | tf_op jit(solution)/shard_map/all_gather | solution.py:50
  221.4 56.5 %fusion.58 = (f32[16,512]{1,0:T(8,128)S(1)}, f32[128,16,512]{2,1,0:T(8,128)S(1)}) fusion(bf16[128,16,512]{2,1,0:T(8,128)(2,1)} %copy.68, bf16[128,512,512]{2,0,1:T(8,128)(2,1)} %all-gather.3.cloned.1.call-done), kind=kOutput, calls=%fused_computation.96 | convolution fusion | flops 1074782208 | bytes 73433088 | tf_op jit(solution)/shard_map/cik,cjk->cij/dot_general | solution.py:51
  279.1 1.5 copy-done.4
  280.6 4.1 convert_reduce_fusion
  286.0 2.7 add_bitcast_fusion
  288.7 3.5 fusion.18
  292.2 2.6 copy.78
  294.9 4.4 copy.75
  299.3 3.8 all-to-all-start
  303.2 3.1 fusion.48
  306.3 43.8 %all-to-all-done = bf16[128,16,512]{0,1,2:T(8,128)(2,1)} async-done(((bf16[128,16,512]{0,1,2:T(8,128)(2,1)}), bf16[128,16,512]{0,1,2:T(8,128)(2,1)}, u32[]{:S(2)}, u32[]{:S(2)}) %all-to-all-start) | async-done | bytes 2097184 | tf_op jit(solution)/shard_map/all_to_all | solution.py:54
  350.1 3.5 copy.77
  353.6 4.9 copy.79
  358.5 152.4 %all-gather.5.cloned.1.call-done = bf16[128,512,512]{2,0,1:T(8,128)(2,1)} async-done(((bf16[128,16,512]{2,0,1:T(8,128)(2,1)}), bf16[128,512,512]{2,0,1:T(8,128)(2,1)}) %all-gather.5.cloned.1.call-update) | async-done | bytes 67108880 | tf_op jit(solution)/shard_map/all_gather | solution.py:55
  510.9 60.0 %fusion.59 = (f32[16,512]{1,0:T(8,128)S(1)}, f32[128,16,512]{2,1,0:T(8,128)}) fusion(bf16[128,512,16]{1,2,0:T(8,128)(2,1)} %copy.79, bf16[128,512,512]{2,0,1:T(8,128)(2,1)} %all-gather.5.cloned.1.call-done), kind=kOutput, calls=%fused_computation.97 | convolution fusion | flops 1074782208 | bytes 73433088 | tf_op jit(solution)/shard_map/cki,ckj->cij/dot_general | solution.py:56
  570.9 2.8 multiply_reduce_fusion
  576.1 3.9 fusion.17
  580.0 3.9 copy.83
  (50 shorter events, 6.2 us)
Async XLA Ops:
  6.5 4.0 copy-start.9
  6.5 4.0 copy-start.8
  6.6 4.0 copy-start.7
  6.6 4.0 copy-start.5
  6.6 214.8 %all-gather.3.cloned.1.call-start = ((), (), s32[]{:S(2)}) async-start(), calls=%async_computation.1 | async-start | bytes 69206016 | tf_op jit(solution)/shard_map/all_gather | solution.py:50
  21.0 4.8 copy-start.10
  21.0 4.8 copy-start.11
  21.0 4.8 copy-start.12
  21.0 4.9 copy-start.6
  21.1 489.8 %all-gather.5.cloned.1.call-start = ((), (), s32[]{:S(2)}) async-start(), calls=%async_computation.2 | async-start | bytes 69206016 | tf_op jit(solution)/shard_map/all_gather | solution.py:55
  278.4 2.2 copy-start.4
  278.4 2.2 copy-start.13
  284.7 1.3 copy-start.1
  294.9 8.3 %copy-start.2 = (bf16[16,512,128]{1,2,0:T(8,128)(2,1)S(1)}, bf16[16,512,128]{1,2,0:T(8,128)(2,1)}, u32[]{:S(2)}) copy-start(bf16[16,512,128]{1,2,0:T(8,128)(2,1)} %copy-done.1) | copy-start | bytes 6291460
  299.3 50.8 %all-to-all-start = ((bf16[128,16,512]{0,1,2:T(8,128)(2,1)}), bf16[128,16,512]{0,1,2:T(8,128)(2,1)}, u32[]{:S(2)}, u32[]{:S(2)}) async-start(bf16[128,16,512]{0,1,2:T(8,128)(2,1)} %copy.75), calls=%async_computation | async-start | bytes 4194304 | tf_op jit(solution)/shard_map/all_to_all | solution.py:54
  570.9 3.5 copy-start
  573.8 2.3 copy-start.3
Sparse Core Ops, SparseCore 0:
  21.2 200.1 all-gather.2
  295.0 215.8 all-gather.4
where the time goes:
time: 596 us; the launch traced here: 591 us
  waiting for transfers between devices  389 us (65%)
  matrix products  136 us (23%)
  local copies, waits for them, and re-layouts  34.5 us (6%)
  between operations  13.9 us (2%)
  other arithmetic  13.6 us (2%)
    all_gather x2, waiting for transfers between devices, local_layers(): right_all = lax.all_gather(right, 'dap', axis=1, tiled=True)  345 us
    dot_general x1, matrix products, local_layers(): jnp.einsum('cki,ckj->cij', left_cols, right_all, preferred_element_type=j...  60 us
    dot_general x1, matrix products, local_layers(): jnp.einsum('cik,cjk->cij', left, right_all, preferred_element_type=jnp.fl...  56.5 us
    all_to_all x1, waiting for transfers between devices, local_layers(): left_cols = lax.all_to_all(left, 'dap', 2, 1, tiled=True)  43.8 us
    convert_element_type x4, local copies, waits for them, and re-layouts, gated_side(): (keep_mask * jax.nn.sigmoid(projected[channels:2 * channels]) * projected...  15.4 us
  transfers between devices with their start and end apart: 3, of which 3 were waited for; matrix products, arithmetic and copies ran while one was open for 4% of the time, Pallas kernels for 0%

commit v1 on v0

v1 whole, which is shorter than its diff:
```python
import functools
import math

import jax
import jax.numpy as jnp
from jax import lax
from jax.experimental import pallas as pl
from jax.experimental.pallas import tpu as pltpu
from jax.sharding import PartitionSpec as P

LN_EPS = 1e-5
LANES = 128
MESH = pl.DeviceIdType.MESH
F32 = jnp.float32
BF16 = jnp.bfloat16


def send_order(side):
    near = [(1, 0), (-1, 0), (0, 1), (0, -1), (2, 0), (0, 2), (1, 1), (-1, -1), (1, -1), (-1, 1), (2, 2), (1, 2),
            (-1, 2), (2, 1), (2, -1), (0, 0)]
    found, order = set(), []
    for dc in range(2):
        for dx, dy in near + [(x, y) for x in range(side) for y in range(side)]:
            offset = (dy % side, dx % side, dc)
            if offset not in found and offset != (0, 0, 0):
                found.add(offset)
                order.append(offset)
    return order


def dot(left, right, dims):
    return lax.dot_general(left, right, (dims, ((), ())), preferred_element_type=F32)


def norm_rows(values, scale, offset):
    count = values.shape[0]
    centred = values - jnp.sum(values, axis=0, keepdims=True) * (1.0 / count)
    variance = jnp.sum(centred * centred, axis=0, keepdims=True) * (1.0 / count)
    return (centred * lax.rsqrt(variance + LN_EPS) * scale + offset).astype(BF16)


def kernel(n, side, slots, pitch, z_ref, mask_ref, wp_ref, bp_ref, wg_ref, wo_ref, vec_ref, out_ref,
           ab_send, ab_recv, o_send, o_recv, stage_a, stage_b, zt, znt, gate, ssem, rsem):
    rows, cols, channels = z_ref.shape
    tiles = cols // LANES
    order = send_order(side)
    me = lax.axis_index("dap")
    core, place = lax.rem(me, 2), me // 2
    my_x, my_y = lax.rem(place, side), place // side

    barrier = pltpu.get_barrier_semaphore()
    for step in range(1, n):
        pl.semaphore_signal(barrier, inc=1, device_id={"dap": lax.rem(me + step, n)}, device_id_type=MESH)

    def peers():
        for dy, dx, dc in order:
            y, x, c = lax.rem(my_y + dy, side), lax.rem(my_x + dx, side), lax.rem(core + dc, 2)
            yield (y * side + x) * 2 + c

    def send_sides(layer, slot):
        target = ab_recv.at[layer, slot, :, pl.ds(pl.multiple_of(me * rows, rows), rows), :]
        phase = 2 * layer
        for peer in peers():
            pltpu.make_async_remote_copy(ab_send.at[slot, peer], target, ssem.at[phase, slot], rsem.at[phase, slot],
                                         device_id={"dap": peer}, device_id_type=MESH).start()
        pltpu.make_async_copy(ab_send.at[slot, me], target, rsem.at[phase, slot]).start()

    def send_sums(layer, slot):
        target = o_recv.at[:, pl.ds(pl.multiple_of((slot * n + me) * pitch, 8), rows), :]
        phase = 2 * layer + 1
        for peer in peers():
            source = o_send.at[slot, :, pl.ds(pl.multiple_of(peer * rows, rows), rows), :]
            pltpu.make_async_remote_copy(source, target, ssem.at[phase, slot], rsem.at[phase, slot],
                                         device_id={"dap": peer}, device_id_type=MESH).start()
        source = o_send.at[slot, :, pl.ds(pl.multiple_of(me * rows, rows), rows), :]
        pltpu.make_async_copy(source, target, rsem.at[phase, slot]).start()

    def wait_bytes(ref, sem):
        pltpu.make_async_copy(ref, ref, sem).wait()

    def wait_sides_sent(layer, slot):
        wait_bytes(ab_send.at[slot, pl.ds(0, n - 1)], ssem.at[2 * layer, slot])

    def wait_sums_sent(layer, slot):
        wait_bytes(o_send.at[slot, :, pl.ds(0, (n - 1) * rows), :], ssem.at[2 * layer + 1, slot])

    def wait_sides(layer, slot):
        wait_bytes(ab_recv.at[layer, slot], rsem.at[2 * layer, slot])

    def wait_sums(layer, slot):
        wait_bytes(o_send.at[slot], rsem.at[2 * layer + 1, slot])

    def make_sides(layer, slot):
        weight = wp_ref[layer, slot]
        bias = bp_ref[layer, slot]

        def row(i, carry):
            projected = dot(weight, znt[i], ((1,), (0,))) + bias
            keep = mask_ref[pl.ds(i, 1), :].astype(F32)
            left = keep * jax.nn.sigmoid(projected[n:2 * n]) * projected[:n]
            right = keep * jax.nn.sigmoid(projected[3 * n:]) * projected[2 * n:3 * n]
            for t in range(tiles):
                stage_a[t, pl.ds(i, n, stride=pitch), :] = left[:, t * LANES:(t + 1) * LANES]
                stage_b[t, pl.ds(i, n, stride=pitch), :] = right[:, t * LANES:(t + 1) * LANES]
            return carry

        lax.fori_loop(0, rows, row, 0)

        def pack(d, carry):
            start = pl.multiple_of(d * pitch, 8)
            for t in range(tiles):
                ab_send[slot, d, 0, :, t * LANES:(t + 1) * LANES] = stage_a[t, pl.ds(start, rows), :].astype(BF16)
                ab_send[slot, d, 1, :, t * LANES:(t + 1) * LANES] = stage_b[t, pl.ds(start, rows), :].astype(BF16)
            return carry

        lax.fori_loop(0, n, pack, 0)

    def make_gates(layer):
        def row(i, carry):
            gate[i] = jax.nn.sigmoid(dot(wg_ref[layer], znt[i], ((1,), (0,))) + vec_ref[layer, 2])
            return carry

        lax.fori_loop(0, rows, row, 0)

    def triangle(layer, slot):
        if layer == 0:
            left = ab_recv[0, slot, 0]
            dims = ((1,), (1,))
        else:
            left = ab_recv[1, slot, 0].T
            dims = ((1,), (0,))
        for t in range(tiles):
            if layer == 0:
                right = ab_recv[0, slot, 1, t * LANES:(t + 1) * LANES, :]
            else:
                right = ab_recv[1, slot, 1, :, t * LANES:(t + 1) * LANES]
            o_send[slot, t] = dot(left, right, dims)

    def finish(layer):
        def row(i, carry):
            for t in range(tiles):
                part = slice(t * LANES, (t + 1) * LANES)
                u = norm_rows(o_recv[t, pl.ds(i, channels, stride=pitch), :], vec_ref[layer, 3], vec_ref[layer, 4])
                update = dot(wo_ref[layer], u, ((1,), (0,))) + vec_ref[layer, 5]
                new = (zt[i, :, part].astype(F32) + gate[i, :, part] * update).astype(BF16)
                if layer == 0:
                    zt[i, :, part] = new
                    znt[i, :, part] = norm_rows(new.astype(F32), vec_ref[1, 0], vec_ref[1, 1])
                else:
                    out_ref[i, part, :] = new.astype(F32).T.astype(BF16)
            return carry

        lax.fori_loop(0, rows, row, 0)

    def first_norm(i, carry):
        values = z_ref[i].astype(F32).T
        zt[i] = values.astype(BF16)
        znt[i] = norm_rows(values, vec_ref[0, 0], vec_ref[0, 1])
        return carry

    lax.fori_loop(0, rows, first_norm, 0)

    for layer in range(2):
        def give_sides(slot, carry):
            if layer == 1:
                wait_sides_sent(0, slot)
            make_sides(layer, slot)
            if layer == 0:
                @pl.when(slot == 0)
                def _():
                    pl.semaphore_wait(barrier, n - 1)
            send_sides(layer, slot)
            return carry

        def give_sums(slot, carry):
            wait_sides(layer, slot)
            if layer == 1:
                wait_sums_sent(0, slot)
            triangle(layer, slot)
            send_sums(layer, slot)
            return carry

        lax.fori_loop(0, slots, give_sides, 0)
        make_gates(layer)
        lax.fori_loop(0, slots, give_sums, 0)
        lax.fori_loop(0, slots, lambda slot, carry: (wait_sums(layer, slot), carry)[1], 0)
        finish(layer)

    def drain(slot, carry):
        wait_sides_sent(1, slot)
        wait_sums_sent(1, slot)
        return carry

    lax.fori_loop(0, slots, drain, 0)


def solution(mesh):
    n = mesh.shape["dap"]
    side = math.isqrt(n // 2)
    row_spec = P(("batch", "dap"), None, None)
    mask_spec = P(("batch", "dap"), None)

    def local_layers(pair, pair_mask, ln_in, w_proj, b_proj, w_gate, b_gate, ln_out, w_out, b_out):
        rows, cols, channels = pair.shape
        slots = channels // n
        tiles = cols // LANES
        pitch = rows + 8
        layers = w_proj.shape[0]

        def by_slot(array):
            split = array.reshape((layers, 4, slots, n) + array.shape[2:])
            return jnp.swapaxes(split, 1, 2).reshape((layers, slots, 4 * n) + array.shape[2:])

        wp = by_slot(jnp.swapaxes(w_proj, 1, 2))
        bp = by_slot(b_proj[..., None]).astype(F32)
        vec = jnp.stack([ln_in[:, 0], ln_in[:, 1], b_gate, ln_out[:, 0], ln_out[:, 1], b_out], axis=1)[..., None].astype(F32)
        vmem = pl.BlockSpec(memory_space=pltpu.VMEM)
        return pl.pallas_call(
            functools.partial(kernel, n, side, slots, pitch),
            out_shape=jax.ShapeDtypeStruct(pair.shape, BF16),
            in_specs=[vmem] * 7,
            out_specs=vmem,
            scratch_shapes=[
                pltpu.VMEM((slots, n, 2, rows, cols), BF16),
                pltpu.VMEM((2, slots, 2, cols, cols), BF16),
                pltpu.VMEM((slots, tiles, cols, LANES), F32),
                pltpu.VMEM((tiles, channels * pitch, LANES), F32),
                pltpu.VMEM((tiles, n * pitch, LANES), F32),
                pltpu.VMEM((tiles, n * pitch, LANES), F32),
                pltpu.VMEM((rows, channels, cols), BF16),
                pltpu.VMEM((rows, channels, cols), BF16),
                pltpu.VMEM((rows, channels, cols), F32),
                pltpu.SemaphoreType.DMA((4, slots)),
                pltpu.SemaphoreType.DMA((4, slots)),
            ],
            compiler_params=pltpu.CompilerParams(collective_id=0, has_side_effects=True, vmem_limit_bytes=60 * 2 ** 20),
            name="triangle_pair",
        )(pair, pair_mask, wp, bp, jnp.swapaxes(w_gate, 1, 2), jnp.swapaxes(w_out, 1, 2), vec)

    return jax.shard_map(local_layers, mesh=mesh,
                         in_specs=(row_spec, mask_spec, P(), P(), P(), P(), P(), P(), P(), P()),
                         out_specs=row_spec, check_vma=False)
```

time: 596 us -> 252 us (0.42)
  waiting for transfers between devices: 389 us -> 0 us
  Pallas kernels: 0 us -> 235 us
  matrix products: 136 us -> 0 us
  local copies, waits for them, and re-layouts: 34.5 us -> 13.5 us
  between operations: 13.9 us -> 0.03 us
  other arithmetic: 13.6 us -> 1 us
    all_gather x2 -> x0, waiting for transfers between devices: 345 us -> none  [local_layers(): right_all = lax.all_gather(right, 'dap', axis=1, tiled=True)]
    pallas_call x0 -> x1, Pallas kernels: none -> 235 us  [local_layers(): pl.pallas_call(functools.partial(kernel, n, side, slots, pitch), out_shap...]
    dot_general x8 -> x0, matrix products: 136 us -> none  [the longest x1 60 us: local_layers(): jnp.einsum('cki,ckj->cij', left_cols, right_all, preferred_element_type=j...]
    all_to_all x1 -> x0, waiting for transfers between devices: 43.8 us -> none  [local_layers(): left_cols = lax.all_to_all(left, 'dap', 2, 1, tiled=True)]
    convert_element_type x5 -> x3, local copies, waits for them, and re-layouts: 19.3 us -> 2.11 us  [local_layers(): bp = by_slot(b_proj[..., None]).astype(F32)]
    all_to_all x2 -> x0, local copies, waits for them, and re-layouts: 8.38 us -> none  [local_layers(): left_cols = lax.all_to_all(left, 'dap', 2, 1, tiled=True)]
    convert_element_type x8 -> x1, other arithmetic: 8.72 us -> 1 us  [local_layers(): jnp.stack([ln_in[:, 0], ln_in[:, 1], b_gate, ln_out[:, 0], ln_out[:, 1],...]
  transfers between devices with their start and end apart: 3 -> 0, of which waited for: 3 -> 0; matrix products, arithmetic and copies ran while one was open for 4% -> 0% of each run, Pallas kernels for 0% -> 0%
where the time goes in v1:
time: 252 us; the launch traced here: 250 us
  Pallas kernels  235 us (93%)
  local copies, waits for them, and re-layouts  13.5 us (5%)
    pallas_call x1, Pallas kernels, local_layers(): pl.pallas_call(functools.partial(kernel, n, side, slots, pitch), out_shap...  235 us
    unnamed x4, local copies, waits for them, and re-layouts  7.35 us

profile of v1, /device:TPU:97, one launch (start us, length us, event | category | flops | bytes accessed | tf_op | source)
XLA Modules:
  0.0 249.7 jit_solution(1553280314021887475)
XLA Ops:
  0.0 0.8 reshape.84
  0.8 1.6 copy.37
  2.3 0.8 copy.40
  3.1 1.6 copy.38
  4.7 0.8 copy.42
  5.5 0.9 copy.39
  6.3 0.9 copy.41
  7.2 1.1 copy.34
  8.3 0.7 copy.35
  9.1 1.0 maximum_convert_fusion.vec_ref
  10.1 1.3 reshape.85.bp_ref
  11.4 235.1 %triangle_pair.1 = bf16[16,512,128]{2,1,0:T(8,128)(2,1)} custom-call(bf16[16,512,128]{2,1,0:T(8,128)(2,1)} %z_ref.1, s32[16,512]{1,0:T(8,128)} %mask_ref.1, bf16[2,4,128,128]{3,2,1,0:T(8,128)(2,1)} %bitcast.17, f32[2,4,128,1]{3,2,1,0:T(8,128)} %reshape.85.bp_ref, bf16[2,128,128]{2,1,0:T(8,128)(2,1)} %bitcast.19, bf16[2,128,128]{2,1,0:T(8,128)(2,1)} %bitcast.20, ...), custom_call_target="tpu_custom_call" | custom-call | tf_op jit(solution)/shard_map/triangle_pair/pallas_call | solution.py:218
  246.6 3.1 %copy.47 = bf16[16,512,128]{2,1,0:T(8,128)(2,1)} copy(bf16[16,512,128]{2,1,0:T(8,128)(2,1)} %triangle_pair.1) | data formatting | bytes 4194304
  (1 shorter events, 0.0 us)

commit v2 on v1

v2 whole, which is shorter than its diff:
```python
import functools
import math

import jax
import jax.numpy as jnp
from jax import lax
from jax.experimental import pallas as pl
from jax.experimental.pallas import tpu as pltpu
from jax.sharding import PartitionSpec as P

LN_EPS = 1e-5
LANES = 128
MESH = pl.DeviceIdType.MESH
F32 = jnp.float32
BF16 = jnp.bfloat16


def send_order(side):
    near = [(1, 0), (-1, 0), (0, 1), (0, -1), (2, 0), (0, 2), (1, 1), (-1, -1), (1, -1), (-1, 1), (2, 2), (1, 2),
            (-1, 2), (2, 1), (2, -1), (0, 0)]
    found, order = set(), []
    for dc in range(2):
        for dx, dy in near + [(x, y) for x in range(side) for y in range(side)]:
            offset = (dy % side, dx % side, dc)
            if offset not in found and offset != (0, 0, 0):
                found.add(offset)
                order.append(offset)
    return order


def dot(left, right, dims):
    return lax.dot_general(left, right, (dims, ((), ())), preferred_element_type=F32)


def norm_rows(values, scale, offset):
    count = values.shape[0]
    centred = values - jnp.sum(values, axis=0, keepdims=True) * (1.0 / count)
    variance = jnp.sum(centred * centred, axis=0, keepdims=True) * (1.0 / count)
    return (centred * lax.rsqrt(variance + LN_EPS) * scale + offset).astype(BF16)


def kernel(n, side, slots, pitch, z_ref, mask_ref, ln_in_ref, w_proj_ref, b_proj_ref, w_gate_ref, b_gate_ref, ln_out_ref,
           w_out_ref, b_out_ref, out_ref, ab_send, ab_recv, o_send, o_recv, stage_a, stage_b, turned, zt, znt, gate,
           wp, bp, wg, wo, vec, keep, ssem, rsem, ssem_part, rsem_part):
    rows, cols, channels = z_ref.shape
    tiles = cols // LANES
    group = 4
    order = send_order(side)
    me = lax.axis_index("dap")
    core, place = lax.rem(me, 2), me // 2
    my_x, my_y = lax.rem(place, side), place // side
    my_rows = pl.ds(pl.multiple_of(me * rows, rows), rows)

    barrier = pltpu.get_barrier_semaphore()
    for step in range(1, n):
        pl.semaphore_signal(barrier, inc=1, device_id={"dap": lax.rem(me + step, n)}, device_id_type=MESH)

    def lanes(t):
        return pl.ds(pl.multiple_of(t * LANES, LANES), LANES)

    def loop(count, body):
        def step(index, carry):
            body(index)
            return carry

        lax.fori_loop(0, count, step, 0)

    def send_all(source_of, target, send_sem, recv_sem):
        for dy, dx, dc in order:
            y, x, c = lax.rem(my_y + dy, side), lax.rem(my_x + dx, side), lax.rem(core + dc, 2)
            peer = (y * side + x) * 2 + c
            pltpu.make_async_remote_copy(source_of(peer), target, send_sem, recv_sem,
                                         device_id={"dap": peer}, device_id_type=MESH).start()
        pltpu.make_async_copy(source_of(me), target, recv_sem).start()

    def wait_bytes(ref, sem):
        pltpu.make_async_copy(ref, ref, sem).wait()

    def send_sides(layer, slot):
        send_all(lambda peer: ab_send.at[slot, peer], ab_recv.at[layer, slot, :, my_rows, :],
                 ssem.at[2 * layer, slot], rsem.at[2 * layer, slot])

    def send_sides_part(layer, t):
        send_all(lambda peer: ab_send.at[0, peer, :, :, lanes(t)], ab_recv.at[layer, 0, :, my_rows, lanes(t)],
                 ssem_part.at[2 * layer, t], rsem_part.at[2 * layer, t])

    def wait_sides(layer, slot):
        wait_bytes(ab_recv.at[layer, slot], rsem.at[2 * layer, slot])

    def wait_sides_part(layer, t):
        wait_bytes(ab_recv.at[layer, 0, :, :, lanes(t)], rsem_part.at[2 * layer, t])

    def wait_sides_sent(layer, slot):
        wait_bytes(ab_send.at[slot, pl.ds(0, n - 1)], ssem.at[2 * layer, slot])

    def wait_sides_sent_part(layer, t):
        wait_bytes(ab_send.at[0, pl.ds(0, n - 1), :, :, lanes(t)], ssem_part.at[2 * layer, t])

    def sum_rows(device):
        return pl.ds(pl.multiple_of(device * rows, rows), rows)

    def sum_target(slot):
        return pl.ds(pl.multiple_of((slot * n + me) * pitch, 8), rows)

    def send_sums(layer, slot):
        send_all(lambda peer: o_send.at[slot, :, sum_rows(peer), :], o_recv.at[:, sum_target(slot), :],
                 ssem.at[2 * layer + 1, slot], rsem.at[2 * layer + 1, slot])

    def send_sums_part(layer, t):
        send_all(lambda peer: o_send.at[slots - 1, t, sum_rows(peer), :], o_recv.at[t, sum_target(slots - 1), :],
                 ssem_part.at[2 * layer + 1, t], rsem_part.at[2 * layer + 1, t])

    def wait_sums(layer, slot):
        wait_bytes(o_send.at[slot], rsem.at[2 * layer + 1, slot])

    def wait_sums_part(layer, t):
        wait_bytes(o_send.at[slots - 1, t], rsem_part.at[2 * layer + 1, t])

    def wait_sums_sent(layer, slot):
        wait_bytes(o_send.at[slot, :, pl.ds(0, (n - 1) * rows), :], ssem.at[2 * layer + 1, slot])

    def wait_sums_sent_part(layer, t):
        wait_bytes(o_send.at[slots - 1, t, pl.ds(0, (n - 1) * rows), :], ssem_part.at[2 * layer + 1, t])

    def column(row):
        return jnp.broadcast_to(row.astype(F32), (LANES, row.shape[-1])).T

    def prepare_first(layer):
        for block in range(4):
            part = slice(block * channels, (block + 1) * channels)
            weight = w_proj_ref[layer, :, part].astype(F32).T.astype(BF16)
            bias = column(b_proj_ref[layer:layer + 1, part])
            for slot in range(slots):
                wp[layer, slot, block * n:(block + 1) * n] = weight[slot * n:(slot + 1) * n]
                bp[layer, slot, block * n:(block + 1) * n] = bias[slot * n:(slot + 1) * n]
        vec[layer, 0] = column(ln_in_ref[layer, 0:1])
        vec[layer, 1] = column(ln_in_ref[layer, 1:2])

    def prepare_rest(layer):
        wg[layer] = w_gate_ref[layer].astype(F32).T.astype(BF16)
        wo[layer] = w_out_ref[layer].astype(F32).T.astype(BF16)
        vec[layer, 2] = column(b_gate_ref[layer:layer + 1])
        vec[layer, 3] = column(ln_out_ref[layer, 0:1])
        vec[layer, 4] = column(ln_out_ref[layer, 1:2])
        vec[layer, 5] = column(b_out_ref[layer:layer + 1])

    def first_norm(t):
        def some(step):
            for k in range(group):
                i = step * group + k
                values = z_ref[i, lanes(t), :].astype(F32).T
                zt[i, :, lanes(t)] = values.astype(BF16)
                znt[i, :, lanes(t)] = norm_rows(values, vec[0, 0], vec[0, 1])

        loop(rows // group, some)

    def gated(layer, slot, pairs):
        normed = jnp.concatenate([znt[i, :, lanes(t)] for i, t in pairs], axis=1)
        projected = dot(wp[layer, slot], normed, ((1,), (0,)))
        bias = bp[layer, slot]
        for k, (i, t) in enumerate(pairs):
            part = projected[:, k * LANES:(k + 1) * LANES] + bias
            kept = keep[t, pl.ds(i, 1), :]
            stage_a[t, pl.ds(i, n, stride=pitch), :] = kept * jax.nn.sigmoid(part[n:2 * n]) * part[:n]
            stage_b[t, pl.ds(i, n, stride=pitch), :] = kept * jax.nn.sigmoid(part[3 * n:]) * part[2 * n:3 * n]

    def pack(slot, tile_list, unroll):
        def some(step):
            for k in range(unroll):
                d = step * unroll + k
                start = pl.multiple_of(d * pitch, 8)
                for t in tile_list:
                    ab_send[slot, d, 0, :, lanes(t)] = stage_a[t, pl.ds(start, rows), :].astype(BF16)
                    ab_send[slot, d, 1, :, lanes(t)] = stage_b[t, pl.ds(start, rows), :].astype(BF16)

        loop(n // unroll, some)

    def make_sides(layer, slot):
        loop(rows, lambda i: gated(layer, slot, [(i, t) for t in range(tiles)]))
        pack(slot, range(tiles), 1)

    def make_sides_part(layer, t):
        loop(rows // group, lambda step: gated(layer, 0, [(step * group + k, t) for k in range(group)]))
        pack(0, [t], 4)

    def make_gates(layer):
        def row(i):
            projected = dot(wg[layer], znt[i], ((1,), (0,)))
            for t in range(tiles):
                part = slice(t * LANES, (t + 1) * LANES)
                gate[i, :, part] = jax.nn.sigmoid(projected[:, part] + vec[layer, 2])

        loop(rows, row)

    def turn(layer, slot):
        if layer == 1:
            turned[...] = ab_recv[1, slot, 0].T

    def triangle(layer, slot, t):
        if layer == 0:
            o_send[slot, t] = dot(ab_recv[0, slot, 0], ab_recv[0, slot, 1, lanes(t), :], ((1,), (1,)))
        else:
            o_send[slot, t] = dot(turned[...], ab_recv[1, slot, 1, :, lanes(t)], ((1,), (0,)))

    def finish(layer, t):
        def some(step):
            places = [step * group + k for k in range(group)]
            normed = [norm_rows(o_recv[t, pl.ds(i, channels, stride=pitch), :], vec[layer, 3], vec[layer, 4]) for i in places]
            update = dot(wo[layer], jnp.concatenate(normed, axis=1), ((1,), (0,)))
            for k, i in enumerate(places):
                added = update[:, k * LANES:(k + 1) * LANES] + vec[layer, 5]
                new = (zt[i, :, lanes(t)].astype(F32) + gate[i, :, lanes(t)] * added).astype(BF16)
                if layer == 0:
                    zt[i, :, lanes(t)] = new
                    znt[i, :, lanes(t)] = norm_rows(new.astype(F32), vec[1, 0], vec[1, 1])
                else:
                    out_ref[i, :, lanes(t)] = new

        loop(rows // group, some)

    prepare_first(0)
    for t in range(tiles):
        keep[t] = mask_ref[:, t * LANES:(t + 1) * LANES].astype(F32)

    def start(t):
        first_norm(t)
        make_sides_part(0, t)

        @pl.when(t == 0)
        def _():
            pl.semaphore_wait(barrier, n - 1)

        send_sides_part(0, t)

    loop(tiles, start)
    for layer in range(2):
        def give_sides(step):
            if layer == 1:
                wait_sides_sent(0, step + 1)
            make_sides(layer, step + 1)
            send_sides(layer, step + 1)

        def give_sums(slot):
            @pl.when(slot == 0)
            def _():
                loop(tiles, lambda t: wait_sides_part(layer, t))

            @pl.when(slot > 0)
            def _():
                wait_sides(layer, slot)

            if layer == 1:
                wait_sums_sent(0, slot)
            turn(layer, slot)
            loop(tiles, lambda t: triangle(layer, slot, t))
            send_sums(layer, slot)

        def give_last_sums(t):
            if layer == 1:
                wait_sums_sent_part(0, t)
            triangle(layer, slots - 1, t)
            send_sums_part(layer, t)

        def take_sums(t):
            wait_sums_part(layer, t)
            finish(layer, t)
            if layer == 0:
                wait_sides_sent_part(0, t)
                make_sides_part(1, t)
                send_sides_part(1, t)

        loop(slots - 1, give_sides)
        if layer == 0:
            prepare_rest(0)
            prepare_first(1)
            prepare_rest(1)
        make_gates(layer)
        loop(slots - 1, give_sums)
        wait_sides(layer, slots - 1)
        turn(layer, slots - 1)
        loop(tiles, give_last_sums)
        loop(slots - 1, lambda slot: wait_sums(layer, slot))
        loop(tiles, take_sums)

    def drain(step):
        wait_sides_sent(1, step + 1)
        wait_sums_sent(1, step)

    def drain_part(t):
        wait_sides_sent_part(1, t)
        wait_sums_sent_part(1, t)

    loop(slots - 1, drain)
    loop(tiles, drain_part)


def solution(mesh):
    n = mesh.shape["dap"]
    side = math.isqrt(n // 2)
    row_spec = P(("batch", "dap"), None, None)
    mask_spec = P(("batch", "dap"), None)

    def local_layers(pair, *others):
        rows, cols, channels = pair.shape
        slots = channels // n
        tiles = cols // LANES
        pitch = rows + 8
        vmem = pl.BlockSpec(memory_space=pltpu.VMEM)
        turned_out = pl.pallas_call(
            functools.partial(kernel, n, side, slots, pitch),
            out_shape=jax.ShapeDtypeStruct((rows, channels, cols), BF16),
            in_specs=[vmem] * (1 + len(others)),
            out_specs=vmem,
            scratch_shapes=[
                pltpu.VMEM((slots, n, 2, rows, cols), BF16),
                pltpu.VMEM((2, slots, 2, cols, cols), BF16),
                pltpu.VMEM((slots, tiles, cols, LANES), F32),
                pltpu.VMEM((tiles, channels * pitch, LANES), F32),
                pltpu.VMEM((tiles, n * pitch, LANES), F32),
                pltpu.VMEM((tiles, n * pitch, LANES), F32),
                pltpu.VMEM((cols, cols), BF16),
                pltpu.VMEM((rows, channels, cols), BF16),
                pltpu.VMEM((rows, channels, cols), BF16),
                pltpu.VMEM((rows, channels, cols), F32),
                pltpu.VMEM((2, slots, 4 * n, channels), BF16),
                pltpu.VMEM((2, slots, 4 * n, LANES), F32),
                pltpu.VMEM((2, channels, channels), BF16),
                pltpu.VMEM((2, channels, channels), BF16),
                pltpu.VMEM((2, 6, channels, LANES), F32),
                pltpu.VMEM((tiles, rows, LANES), F32),
                pltpu.SemaphoreType.DMA((4, slots)),
                pltpu.SemaphoreType.DMA((4, slots)),
                pltpu.SemaphoreType.DMA((4, tiles)),
                pltpu.SemaphoreType.DMA((4, tiles)),
            ],
            compiler_params=pltpu.CompilerParams(collective_id=0, has_side_effects=True, vmem_limit_bytes=60 * 2 ** 20),
            name="triangle_pair",
        )(pair, *others)
        return jnp.swapaxes(turned_out, 1, 2)

    return jax.shard_map(local_layers, mesh=mesh,
                         in_specs=(row_spec, mask_spec, P(), P(), P(), P(), P(), P(), P(), P()),
                         out_specs=row_spec, check_vma=False)
```

time: 252 us -> 225 us (0.89)
  the two profiles are of different devices: /device:TPU:97 before, /device:TPU:99 now
where the time goes in v2:
time: 225 us
  Pallas kernels  221 us (98%)
  local copies, waits for them, and re-layouts  3.91 us (2%)
    pallas_call x1, Pallas kernels, local_layers(): pl.pallas_call(functools.partial(kernel, n, side, slots, pitch), out_shap...  221 us

profile of v2, /device:TPU:99, one launch (start us, length us, event | category | flops | bytes accessed | tf_op | source)
XLA Modules:
  0.0 224.7 jit_solution(11582345726309109099)
XLA Ops:
  0.0 220.8 %triangle_pair.1 = bf16[16,128,512]{2,1,0:T(8,128)(2,1)} custom-call(bf16[16,512,128]{2,1,0:T(8,128)(2,1)} %z_ref.1, s32[16,512]{1,0:T(8,128)} %mask_ref.1, bf16[2,2,128]{2,1,0:T(2,128)(2,1)} %ln_in_ref.1, bf16[2,128,512]{2,1,0:T(8,128)(2,1)} %w_proj_ref.1, bf16[2,512]{1,0:T(2,128)(2,1)} %b_proj_ref.1, bf16[2,128,128]{2,1,0:T(8,128)(2,1)} %w_gate_ref.1, ...), custom_call_target="tpu_custom_call" | custom-call | tf_op jit(solution)/shard_map/triangle_pair/pallas_call | solution.py:309
  220.8 3.9 %copy.11 = bf16[16,512,128]{2,1,0:T(8,128)(2,1)} copy(bf16[16,512,128]{1,2,0:T(8,128)(2,1)} %bitcast.1) | data formatting | bytes 4194304 | tf_op jit(solution)/shard_map/transpose | solution.py:339

commit v3 on v2

--- a/solution.py
+++ b/solution.py
@@ -41,7 +41,7 @@
 
 def kernel(n, side, slots, pitch, z_ref, mask_ref, ln_in_ref, w_proj_ref, b_proj_ref, w_gate_ref, b_gate_ref, ln_out_ref,
            w_out_ref, b_out_ref, out_ref, ab_send, ab_recv, o_send, o_recv, stage_a, stage_b, turned, zt, znt, gate,
-           wp, bp, wg, wo, vec, keep, ssem, rsem, ssem_part, rsem_part):
+           wp, bp, wg, wo, vec, keep, sides_sent, sides_here, sums_sent, sums_here):
     rows, cols, channels = z_ref.shape
     tiles = cols // LANES
     group = 4
@@ -76,51 +76,26 @@
     def wait_bytes(ref, sem):
         pltpu.make_async_copy(ref, ref, sem).wait()
 
-    def send_sides(layer, slot):
-        send_all(lambda peer: ab_send.at[slot, peer], ab_recv.at[layer, slot, :, my_rows, :],
-                 ssem.at[2 * layer, slot], rsem.at[2 * layer, slot])
-
-    def send_sides_part(layer, t):
-        send_all(lambda peer: ab_send.at[0, peer, :, :, lanes(t)], ab_recv.at[layer, 0, :, my_rows, lanes(t)],
-                 ssem_part.at[2 * layer, t], rsem_part.at[2 * layer, t])
+    def send_sides(layer, slot, t):
+        send_all(lambda peer: ab_send.at[slot, peer, :, :, lanes(t)], ab_recv.at[layer, slot, :, my_rows, lanes(t)],
+                 sides_sent.at[layer, slot], sides_here.at[layer, slot])
 
     def wait_sides(layer, slot):
-        wait_bytes(ab_recv.at[layer, slot], rsem.at[2 * layer, slot])
-
-    def wait_sides_part(layer, t):
-        wait_bytes(ab_recv.at[layer, 0, :, :, lanes(t)], rsem_part.at[2 * layer, t])
+        wait_bytes(ab_recv.at[layer, slot], sides_here.at[layer, slot])
 
     def wait_sides_sent(layer, slot):
-        wait_bytes(ab_send.at[slot, pl.ds(0, n - 1)], ssem.at[2 * layer, slot])
-
-    def wait_sides_sent_part(layer, t):
-        wait_bytes(ab_send.at[0, pl.ds(0, n - 1), :, :, lanes(t)], ssem_part.at[2 * layer, t])
-
-    def sum_rows(device):
-        return pl.ds(pl.multiple_of(device * rows, rows), rows)
-
-    def sum_target(slot):
-        return pl.ds(pl.multiple_of((slot * n + me) * pitch, 8), rows)
-
-    def send_sums(layer, slot):
-        send_all(lambda peer: o_send.at[slot, :, sum_rows(peer), :], o_recv.at[:, sum_target(slot), :],
-                 ssem.at[2 * layer + 1, slot], rsem.at[2 * layer + 1, slot])
-
-    def send_sums_part(layer, t):
-        send_all(lambda peer: o_send.at[slots - 1, t, sum_rows(peer), :], o_recv.at[t, sum_target(slots - 1), :],
-                 ssem_part.at[2 * layer + 1, t], rsem_part.at[2 * layer + 1, t])
-
-    def wait_sums(layer, slot):
-        wait_bytes(o_send.at[slot], rsem.at[2 * layer + 1, slot])
-
-    def wait_sums_part(layer, t):
-        wait_bytes(o_send.at[slots - 1, t], rsem_part.at[2 * layer + 1, t])
-
-    def wait_sums_sent(layer, slot):
-        wait_bytes(o_send.at[slot, :, pl.ds(0, (n - 1) * rows), :], ssem.at[2 * layer + 1, slot])
-
-    def wait_sums_sent_part(layer, t):
-        wait_bytes(o_send.at[slots - 1, t, pl.ds(0, (n - 1) * rows), :], ssem_part.at[2 * layer + 1, t])
+        wait_bytes(ab_send.at[slot, pl.ds(0, n - 1)], sides_sent.at[layer, slot])
+
+    def send_sums(layer, slot, t):
+        send_all(lambda peer: o_send.at[t, slot, pl.ds(pl.multiple_of(peer * rows, rows), rows), :],
+                 o_recv.at[t, pl.ds(pl.multiple_of((slot * n + me) * pitch, 8), rows), :],
+                 sums_sent.at[layer, t], sums_here.at[layer, t])
+
+    def wait_sums(layer, t):
+        wait_bytes(o_send.at[t], sums_here.at[layer, t])
+
+    def wait_sums_sent(layer, t):
+        wait_bytes(o_send.at[t, :, pl.ds(0, (n - 1) * rows), :], sums_sent.at[layer, t])
 
     def column(row):
         return jnp.broadcast_to(row.astype(F32), (LANES, row.shape[-1])).T
@@ -198,9 +173,9 @@
 
     def triangle(layer, slot, t):
         if layer == 0:
-            o_send[slot, t] = dot(ab_recv[0, slot, 0], ab_recv[0, slot, 1, lanes(t), :], ((1,), (1,)))
+            o_send[t, slot] = dot(ab_recv[0, slot, 0], ab_recv[0, slot, 1, lanes(t), :], ((1,), (1,)))
         else:
-            o_send[slot, t] = dot(turned[...], ab_recv[1, slot, 1, :, lanes(t)], ((1,), (0,)))
+            o_send[t, slot] = dot(turned[...], ab_recv[1, slot, 1, :, lanes(t)], ((1,), (0,)))
 
     def finish(layer, t):
         def some(step):
@@ -230,7 +205,7 @@
         def _():
             pl.semaphore_wait(barrier, n - 1)
 
-        send_sides_part(0, t)
+        send_sides(0, 0, t)
 
     loop(tiles, start)
     for layer in range(2):
@@ -238,36 +213,24 @@
             if layer == 1:
                 wait_sides_sent(0, step + 1)
             make_sides(layer, step + 1)
-            send_sides(layer, step + 1)
+            loop(tiles, lambda t: send_sides(layer, step + 1, t))
 
         def give_sums(slot):
-            @pl.when(slot == 0)
-            def _():
-                loop(tiles, lambda t: wait_sides_part(layer, t))
-
-            @pl.when(slot > 0)
-            def _():
-                wait_sides(layer, slot)
-
-            if layer == 1:
-                wait_sums_sent(0, slot)
+            wait_sides(layer, slot)
             turn(layer, slot)
-            loop(tiles, lambda t: triangle(layer, slot, t))
-            send_sums(layer, slot)
-
-        def give_last_sums(t):
-            if layer == 1:
-                wait_sums_sent_part(0, t)
-            triangle(layer, slots - 1, t)
-            send_sums_part(layer, t)
+
+            def some(t):
+                triangle(layer, slot, t)
+                send_sums(layer, slot, t)
+
+            loop(tiles, some)
 
         def take_sums(t):
-            wait_sums_part(layer, t)
+            wait_sums(layer, t)
             finish(layer, t)
             if layer == 0:
-                wait_sides_sent_part(0, t)
                 make_sides_part(1, t)
-                send_sides_part(1, t)
+                send_sides(1, 0, t)
 
         loop(slots - 1, give_sides)
         if layer == 0:
@@ -275,23 +238,15 @@
             prepare_first(1)
             prepare_rest(1)
         make_gates(layer)
-        loop(slots - 1, give_sums)
-        wait_sides(layer, slots - 1)
-        turn(layer, slots - 1)
-        loop(tiles, give_last_sums)
-        loop(slots - 1, lambda slot: wait_sums(layer, slot))
+        if layer == 1:
+            loop(tiles, lambda t: wait_sums_sent(0, t))
+        loop(slots, give_sums)
+        if layer == 0:
+            wait_sides_sent(0, 0)
         loop(tiles, take_sums)
 
-    def drain(step):
-        wait_sides_sent(1, step + 1)
-        wait_sums_sent(1, step)
-
-    def drain_part(t):
-        wait_sides_sent_part(1, t)
-        wait_sums_sent_part(1, t)
-
-    loop(slots - 1, drain)
-    loop(tiles, drain_part)
+    loop(slots, lambda slot: wait_sides_sent(1, slot))
+    loop(tiles, lambda t: wait_sums_sent(1, t))
 
 
 def solution(mesh):
@@ -314,7 +269,7 @@
             scratch_shapes=[
                 pltpu.VMEM((slots, n, 2, rows, cols), BF16),
                 pltpu.VMEM((2, slots, 2, cols, cols), BF16),
-                pltpu.VMEM((slots, tiles, cols, LANES), F32),
+                pltpu.VMEM((tiles, slots, cols, LANES), F32),
                 pltpu.VMEM((tiles, channels * pitch, LANES), F32),
                 pltpu.VMEM((tiles, n * pitch, LANES), F32),
                 pltpu.VMEM((tiles, n * pitch, LANES), F32),
@@ -328,10 +283,10 @@
                 pltpu.VMEM((2, channels, channels), BF16),
                 pltpu.VMEM((2, 6, channels, LANES), F32),
                 pltpu.VMEM((tiles, rows, LANES), F32),
-                pltpu.SemaphoreType.DMA((4, slots)),
-                pltpu.SemaphoreType.DMA((4, slots)),
-                pltpu.SemaphoreType.DMA((4, tiles)),
-                pltpu.SemaphoreType.DMA((4, tiles)),
+                pltpu.SemaphoreType.DMA((2, slots)),
+                pltpu.SemaphoreType.DMA((2, slots)),
+                pltpu.SemaphoreType.DMA((2, tiles)),
+                pltpu.SemaphoreType.DMA((2, tiles)),
             ],
             compiler_params=pltpu.CompilerParams(collective_id=0, has_side_effects=True, vmem_limit_bytes=60 * 2 ** 20),
             name="triangle_pair",

time: 225 us -> 200 us (0.89)
  the two profiles are of different devices: /device:TPU:99 before, /device:TPU:97 now
where the time goes in v3:
time: 200 us
  Pallas kernels  196 us (98%)
  local copies, waits for them, and re-layouts  3.91 us (2%)
    pallas_call x1, Pallas kernels, local_layers(): pl.pallas_call(functools.partial(kernel, n, side, slots, pitch), out_shap...  196 us

profile of v3, /device:TPU:97, one launch (start us, length us, event | category | flops | bytes accessed | tf_op | source)
XLA Modules:
  0.0 200.0 jit_solution(17245825278913889554)
XLA Ops:
  0.0 196.1 %triangle_pair.1 = bf16[16,128,512]{2,1,0:T(8,128)(2,1)} custom-call(bf16[16,512,128]{2,1,0:T(8,128)(2,1)} %z_ref.1, s32[16,512]{1,0:T(8,128)} %mask_ref.1, bf16[2,2,128]{2,1,0:T(2,128)(2,1)} %ln_in_ref.1, bf16[2,128,512]{2,1,0:T(8,128)(2,1)} %w_proj_ref.1, bf16[2,512]{1,0:T(2,128)(2,1)} %b_proj_ref.1, bf16[2,128,128]{2,1,0:T(8,128)(2,1)} %w_gate_ref.1, ...), custom_call_target="tpu_custom_call" | custom-call | tf_op jit(solution)/shard_map/triangle_pair/pallas_call | solution.py:264
  196.1 3.9 %copy.11 = bf16[16,512,128]{2,1,0:T(8,128)(2,1)} copy(bf16[16,512,128]{1,2,0:T(8,128)(2,1)} %bitcast.1) | data formatting | bytes 4194304 | tf_op jit(solution)/shard_map/transpose | solution.py:294

commit v4 on v3

--- a/solution.py
+++ b/solution.py
@@ -39,8 +39,9 @@
     return (centred * lax.rsqrt(variance + LN_EPS) * scale + offset).astype(BF16)
 
 
-def kernel(n, side, slots, pitch, z_ref, mask_ref, ln_in_ref, w_proj_ref, b_proj_ref, w_gate_ref, b_gate_ref, ln_out_ref,
-           w_out_ref, b_out_ref, out_ref, ab_send, ab_recv, o_send, o_recv, stage_a, stage_b, turned, zt, znt, gate,
+def kernel(n, side, slots, pitch, z_hbm, mask_hbm, ln_in_hbm, w_proj_hbm, b_proj_hbm, w_gate_hbm, b_gate_hbm, ln_out_hbm,
+           w_out_hbm, b_out_hbm, out_ref, z_ref, mask_ref, ln_in_ref, w_proj_ref, b_proj_ref, w_gate_ref, b_gate_ref, ln_out_ref,
+           w_out_ref, b_out_ref, z_here, weight_here, ab_send, ab_recv, o_send, o_recv, stage_a, stage_b, turned, zt, znt, gate,
            wp, bp, wg, wo, vec, keep, sides_sent, sides_here, sums_sent, sums_here):
     rows, cols, channels = z_ref.shape
     tiles = cols // LANES
@@ -50,6 +51,24 @@
     core, place = lax.rem(me, 2), me // 2
     my_x, my_y = lax.rem(place, side), place // side
     my_rows = pl.ds(pl.multiple_of(me * rows, rows), rows)
+
+    first_weights = [(w_proj_hbm, w_proj_ref), (b_proj_hbm, b_proj_ref), (ln_in_hbm, ln_in_ref), (mask_hbm, mask_ref)]
+    rest_weights = [(w_gate_hbm, w_gate_ref), (b_gate_hbm, b_gate_ref), (ln_out_hbm, ln_out_ref), (w_out_hbm, w_out_ref),
+                    (b_out_hbm, b_out_ref)]
+    first_copies, rest_copies = [
+        [pltpu.make_async_copy(source, target, weight_here.at[base + k]) for k, (source, target) in enumerate(group_refs)]
+        for base, group_refs in ((0, first_weights), (len(first_weights), rest_weights))]
+
+    def z_copy(t):
+        part = pl.ds(pl.multiple_of(t * LANES, LANES), LANES)
+        return pltpu.make_async_copy(z_hbm.at[:, part, :], z_ref.at[:, part, :], z_here.at[t])
+
+    for copy in first_copies:
+        copy.start()
+    for t in range(tiles):
+        z_copy(t).start()
+    for copy in rest_copies:
+        copy.start()
 
     barrier = pltpu.get_barrier_semaphore()
     for step in range(1, n):
@@ -189,15 +208,18 @@
                     zt[i, :, lanes(t)] = new
                     znt[i, :, lanes(t)] = norm_rows(new.astype(F32), vec[1, 0], vec[1, 1])
                 else:
-                    out_ref[i, :, lanes(t)] = new
+                    out_ref[i, lanes(t), :] = new.astype(F32).T.astype(BF16)
 
         loop(rows // group, some)
 
+    for copy in first_copies:
+        copy.wait()
     prepare_first(0)
     for t in range(tiles):
         keep[t] = mask_ref[:, t * LANES:(t + 1) * LANES].astype(F32)
 
     def start(t):
+        z_copy(t).wait()
         first_norm(t)
         make_sides_part(0, t)
 
@@ -234,6 +256,8 @@
 
         loop(slots - 1, give_sides)
         if layer == 0:
+            for copy in rest_copies:
+                copy.wait()
             prepare_rest(0)
             prepare_first(1)
             prepare_rest(1)
@@ -260,13 +284,15 @@
         slots = channels // n
         tiles = cols // LANES
         pitch = rows + 8
-        vmem = pl.BlockSpec(memory_space=pltpu.VMEM)
-        turned_out = pl.pallas_call(
+        operands = (pair,) + others
+        return pl.pallas_call(
             functools.partial(kernel, n, side, slots, pitch),
-            out_shape=jax.ShapeDtypeStruct((rows, channels, cols), BF16),
-            in_specs=[vmem] * (1 + len(others)),
-            out_specs=vmem,
-            scratch_shapes=[
+            out_shape=pltpu.VMEM(pair.shape, BF16),
+            in_specs=[pl.BlockSpec(memory_space=pltpu.HBM)] * len(operands),
+            out_specs=pl.BlockSpec(memory_space=pltpu.VMEM),
+            scratch_shapes=[pltpu.VMEM(operand.shape, operand.dtype) for operand in operands] + [
+                pltpu.SemaphoreType.DMA((tiles,)),
+                pltpu.SemaphoreType.DMA((len(operands) - 1,)),
                 pltpu.VMEM((slots, n, 2, rows, cols), BF16),
                 pltpu.VMEM((2, slots, 2, cols, cols), BF16),
                 pltpu.VMEM((tiles, slots, cols, LANES), F32),
@@ -288,10 +314,9 @@
                 pltpu.SemaphoreType.DMA((2, tiles)),
                 pltpu.SemaphoreType.DMA((2, tiles)),
             ],
-            compiler_params=pltpu.CompilerParams(collective_id=0, has_side_effects=True, vmem_limit_bytes=60 * 2 ** 20),
+            compiler_params=pltpu.CompilerParams(collective_id=0, has_side_effects=True, vmem_limit_bytes=54 * 2 ** 20),
             name="triangle_pair",
-        )(pair, *others)
-        return jnp.swapaxes(turned_out, 1, 2)
+        )(*operands)
 
     return jax.shard_map(local_layers, mesh=mesh,
                          in_specs=(row_spec, mask_spec, P(), P(), P(), P(), P(), P(), P(), P()),

time: 200 us -> 195 us (0.975)
  Pallas kernels: 196 us -> 193 us
  local copies, waits for them, and re-layouts: 3.91 us -> 1.32 us
    transpose x1 -> x0, local copies, waits for them, and re-layouts: 3.91 us -> none  [local_layers(): return jnp.swapaxes(turned_out, 1, 2)]
    pallas_call x1, Pallas kernels: 196 us -> 193 us  [local_layers(): pl.pallas_call(functools.partial(kernel, n, side, slots, pitch), out_shap...]
where the time goes in v4:
time: 195 us
  Pallas kernels  193 us (99%)
    pallas_call x1, Pallas kernels, local_layers(): pl.pallas_call(functools.partial(kernel, n, side, slots, pitch), out_shap...  193 us

profile of v4, /device:TPU:97, one launch (start us, length us, event | category | flops | bytes accessed | tf_op | source)
XLA Modules:
  0.0 194.8 jit_solution(5448960103802015389)
XLA Ops:
  0.0 193.4 %triangle_pair.1 = bf16[16,512,128]{2,1,0:T(8,128)(2,1)S(1)} custom-call(bf16[16,512,128]{2,1,0:T(8,128)(2,1)} %z_hbm.1, s32[16,512]{1,0:T(8,128)} %mask_hbm.1, bf16[2,2,128]{2,1,0:T(2,128)(2,1)} %ln_in_hbm.1, bf16[2,128,512]{2,1,0:T(8,128)(2,1)} %w_proj_hbm.1, bf16[2,512]{1,0:T(2,128)(2,1)} %b_proj_hbm.1, bf16[2,128,128]{2,1,0:T(8,128)(2,1)} %w_gate_hbm.1, ...), custom_call_target="tpu_custom_call" | custom-call | tf_op jit(solution)/shard_map/triangle_pair/pallas_call | solution.py:288
  193.5 1.3 copy.12

commit v5 on v4

--- a/solution.py
+++ b/solution.py
@@ -28,6 +28,13 @@
     return order
 
 
+def group_order(side):
+    ring = [step % side for step in (1, -1)] + [0] + [step % side for step in (1, -1)] + [2 % side, 2 % side, 0]
+    flips = [0, 0, 1, 1, 1, 0, 1, 0]
+    return [(unit, step, flip, dc) for dc in range(2) for step, flip in zip(ring, flips) for unit in range(2)
+            if (step, flip, dc) != (0, 0, 0)]
+
+
 def dot(left, right, dims):
     return lax.dot_general(left, right, (dims, ((), ())), preferred_element_type=F32)
 
@@ -41,8 +48,8 @@
 
 def kernel(n, side, slots, pitch, z_hbm, mask_hbm, ln_in_hbm, w_proj_hbm, b_proj_hbm, w_gate_hbm, b_gate_hbm, ln_out_hbm,
            w_out_hbm, b_out_hbm, out_ref, z_ref, mask_ref, ln_in_ref, w_proj_ref, b_proj_ref, w_gate_ref, b_gate_ref, ln_out_ref,
-           w_out_ref, b_out_ref, z_here, weight_here, ab_send, ab_recv, o_send, o_recv, stage_a, stage_b, turned, zt, znt, gate,
-           wp, bp, wg, wo, vec, keep, sides_sent, sides_here, sums_sent, sums_here):
+           w_out_ref, b_out_ref, z_here, weight_here, ab_send, a_first, b_first, ab_recv, o_send, o_recv, stage_a, stage_b, turned, zt, znt, gate,
+           wp, bp, wg, wo, vec, keep, sides_sent, sides_here, sums_sent, sums_here, twin_sent, twin_here):
     rows, cols, channels = z_ref.shape
     tiles = cols // LANES
     group = 4
@@ -95,15 +102,105 @@
     def wait_bytes(ref, sem):
         pltpu.make_async_copy(ref, ref, sem).wait()
 
+    half = n // 2
+
+    def place_of(unit, slot):
+        along, across = (my_y, my_x) if unit == 0 else (my_x, my_y)
+        shift = lax.rem(slot, 2)
+        turned_along = lax.rem(along + shift, side)
+        return shift, turned_along, turned_along // 2, across
+
+    def entry(unit, turned_along, pair, across, c):
+        return unit * half + (lax.rem(turned_along + pair, 2) * side + across) * 2 + c
+
+    def device(unit, turned_along, shift, across, c):
+        along = lax.rem(turned_along + side - shift, side)
+        return ((along * side + across) if unit == 0 else (across * side + along)) * 2 + c
+
+    def my_entries(slot):
+        entries = []
+        for unit in range(2):
+            shift, turned_along, pair, across = place_of(unit, slot)
+            entries.append(entry(unit, turned_along, pair, across, core))
+        return entries
+
+    def group_peers(couple):
+        for unit, step, flip, dc in group_order(side):
+            for slot in couple:
+                shift, turned_along, pair, across = place_of(unit, slot)
+                there = turned_along + (1 - 2 * (turned_along - 2 * pair)) if flip else turned_along
+                across_there, c = lax.rem(across + step, side), lax.rem(core + dc, 2)
+                yield slot, unit, entry(unit, there, pair, across_there, c), device(unit, there, shift, across_there, c)
+
+    def couple_of(step):
+        return 2 * step, 2 * step + 1
+
+    def entry_rows(index):
+        return pl.ds(pl.multiple_of(index * rows, rows), rows)
+
+    def send_first_sides(step, t, width):
+        part = pl.ds(pl.multiple_of(t * LANES, LANES), width)
+        couple = couple_of(step)
+
+        def copies(slot, unit, index, mine):
+            return ((ab_send.at[slot, index, 0, :, part], a_first.at[slot, entry_rows(mine), part]),
+                    (ab_send.at[slot, index, 1, :, part], b_first.at[slot, unit, my_rows, part]))
+
+        entries = [my_entries(slot) for slot in couple]
+        for count, (slot, unit, index, peer) in enumerate(group_peers(couple)):
+            for source, target in copies(slot, unit, index, entries[count % 2][unit]):
+                pltpu.make_async_remote_copy(source, target, sides_sent.at[0, slot], sides_here.at[0, slot],
+                                             device_id={"dap": peer}, device_id_type=MESH).start()
+        for slot, mine in zip(couple, entries):
+            for unit in range(2):
+                for source, target in copies(slot, unit, mine[unit], mine[unit]):
+                    pltpu.make_async_copy(source, target, sides_here.at[0, slot]).start()
+
+    def wait_first_sides(slot):
+        wait_bytes(b_first.at[slot], sides_here.at[0, slot])
+
+    def send_to_twin(step):
+        for other in range(side):
+            for k in range(2):
+                for unit in range(2):
+                    for slot in couple_of(step):
+                        shift, turned_along, pair, across = place_of(unit, slot)
+                        twin = device(unit, side - 1 - turned_along, shift, across, core)
+                        chip = device(unit, 2 * pair + k, shift, other, 0)
+                        block = pl.ds(pl.multiple_of(chip * rows, 2 * rows), 2 * rows)
+                        pltpu.make_async_remote_copy(b_first.at[slot, unit, block, :], b_first.at[slot, unit, block, :],
+                                                     twin_sent.at[slot], twin_here.at[slot],
+                                                     device_id={"dap": twin}, device_id_type=MESH).start()
+
+    def wait_twin(slot, sem):
+        wait_bytes(a_first.at[slot], sem.at[slot])
+
+    def send_first_sums(step, t):
+        couple = couple_of(step)
+        sent, here = sums_sent.at[0, t], sums_here.at[0, t]
+
+        def ends(slot, index, mine):
+            return (o_send.at[t, slot, entry_rows(index), :],
+                    o_recv.at[t, pl.ds(pl.multiple_of((slot * n + mine) * pitch, 8), rows), :])
+
+        entries = [my_entries(slot) for slot in couple]
+        for count, (slot, unit, index, peer) in enumerate(group_peers(couple)):
+            source, target = ends(slot, index, entries[count % 2][unit])
+            pltpu.make_async_remote_copy(source, target, sent, here, device_id={"dap": peer}, device_id_type=MESH).start()
+        for slot, mine in zip(couple, entries):
+            for unit in range(2):
+                source, target = ends(slot, mine[unit], mine[unit])
+                pltpu.make_async_copy(source, target, here).start()
+
     def send_sides(layer, slot, t):
-        send_all(lambda peer: ab_send.at[slot, peer, :, :, lanes(t)], ab_recv.at[layer, slot, :, my_rows, lanes(t)],
+        send_all(lambda peer: ab_send.at[slot, peer, :, :, lanes(t)], ab_recv.at[slot, :, my_rows, lanes(t)],
                  sides_sent.at[layer, slot], sides_here.at[layer, slot])
 
     def wait_sides(layer, slot):
-        wait_bytes(ab_recv.at[layer, slot], sides_here.at[layer, slot])
+        wait_bytes(ab_recv.at[slot], sides_here.at[layer, slot])
 
     def wait_sides_sent(layer, slot):
-        wait_bytes(ab_send.at[slot, pl.ds(0, n - 1)], sides_sent.at[layer, slot])
+        wait_bytes(ab_send.at[slot, pl.ds(0, n - 2 + layer)], sides_sent.at[layer, slot])
 
     def send_sums(layer, slot, t):
         send_all(lambda peer: o_send.at[t, slot, pl.ds(pl.multiple_of(peer * rows, rows), rows), :],
@@ -114,7 +211,7 @@
         wait_bytes(o_send.at[t], sums_here.at[layer, t])
 
     def wait_sums_sent(layer, t):
-        wait_bytes(o_send.at[t, :, pl.ds(0, (n - 1) * rows), :], sums_sent.at[layer, t])
+        wait_bytes(o_send.at[t, :, pl.ds(0, (n - 2 + layer) * rows), :], sums_sent.at[layer, t])
 
     def column(row):
         return jnp.broadcast_to(row.astype(F32), (LANES, row.shape[-1])).T
@@ -173,9 +270,13 @@
         loop(rows, lambda i: gated(layer, slot, [(i, t) for t in range(tiles)]))
         pack(slot, range(tiles), 1)
 
-    def make_sides_part(layer, t):
-        loop(rows // group, lambda step: gated(layer, 0, [(step * group + k, t) for k in range(group)]))
-        pack(0, [t], 4)
+    def make_sides_part(layer, slot, t):
+        loop(rows // group, lambda step: gated(layer, slot, [(step * group + k, t) for k in range(group)]))
+        pack(slot, [t], 4)
+
+    def make_sides_half(layer, slot, t):
+        loop(rows // 2, lambda step: gated(layer, slot, [(2 * step + k, t + j) for k in range(2) for j in range(2)]))
+        pack(slot, [t, t + 1], 2)
 
     def make_gates(layer):
         def row(i):
@@ -188,13 +289,15 @@
 
     def turn(layer, slot):
         if layer == 1:
-            turned[...] = ab_recv[1, slot, 0].T
+            turned[...] = ab_recv[slot, 0].T
 
     def triangle(layer, slot, t):
         if layer == 0:
-            o_send[t, slot] = dot(ab_recv[0, slot, 0], ab_recv[0, slot, 1, lanes(t), :], ((1,), (1,)))
+            for unit in range(2):
+                part = slice(unit * half * rows, (unit + 1) * half * rows)
+                o_send[t, slot, part] = dot(a_first[slot, part], b_first[slot, unit, lanes(t), :], ((1,), (1,)))
         else:
-            o_send[t, slot] = dot(turned[...], ab_recv[1, slot, 1, :, lanes(t)], ((1,), (0,)))
+            o_send[t, slot] = dot(turned[...], ab_recv[slot, 1, :, lanes(t)], ((1,), (0,)))
 
     def finish(layer, t):
         def some(step):
@@ -221,29 +324,44 @@
     def start(t):
         z_copy(t).wait()
         first_norm(t)
-        make_sides_part(0, t)
+        make_sides_part(0, 0, t)
+        make_sides_part(0, 1, t)
 
         @pl.when(t == 0)
         def _():
             pl.semaphore_wait(barrier, n - 1)
 
-        send_sides(0, 0, t)
+        send_first_sides(0, t, LANES)
 
     loop(tiles, start)
     for layer in range(2):
         def give_sides(step):
-            if layer == 1:
-                wait_sides_sent(0, step + 1)
-            make_sides(layer, step + 1)
-            loop(tiles, lambda t: send_sides(layer, step + 1, t))
+            wait_sides_sent(0, step + 1)
+            make_sides(1, step + 1)
+            loop(tiles, lambda t: send_sides(1, step + 1, t))
+
+        def give_first_sums(step):
+            for slot in couple_of(step):
+                wait_twin(slot, twin_here)
+
+            def some(t):
+                for slot in couple_of(step):
+                    triangle(0, slot, t)
+                send_first_sums(step, t)
+
+                @pl.when((t == tiles // 2 - 1) & (step < slots // 2 - 1))
+                def _():
+                    forward(step + 1)
+
+            loop(tiles, some)
 
         def give_sums(slot):
-            wait_sides(layer, slot)
-            turn(layer, slot)
+            wait_sides(1, slot)
+            turn(1, slot)
 
             def some(t):
-                triangle(layer, slot, t)
-                send_sums(layer, slot, t)
+                triangle(1, slot, t)
+                send_sums(1, slot, t)
 
             loop(tiles, some)
 
@@ -251,24 +369,42 @@
             wait_sums(layer, t)
             finish(layer, t)
             if layer == 0:
-                make_sides_part(1, t)
+                make_sides_part(1, 0, t)
                 send_sides(1, 0, t)
 
-        loop(slots - 1, give_sides)
+        def forward(step):
+            for slot in couple_of(step):
+                wait_first_sides(slot)
+            send_to_twin(step)
+
         if layer == 0:
+            def give_first_sides(index):
+                step, t = 1 + index // (tiles // 2), 2 * lax.rem(index, tiles // 2)
+                for slot in couple_of(step):
+                    make_sides_half(0, slot, t)
+                send_first_sides(step, t, 2 * LANES)
+
+                @pl.when(index == 1)
+                def _():
+                    forward(0)
+
+            loop((slots // 2 - 1) * (tiles // 2), give_first_sides)
             for copy in rest_copies:
                 copy.wait()
             prepare_rest(0)
             prepare_first(1)
             prepare_rest(1)
-        make_gates(layer)
-        if layer == 1:
+            make_gates(0)
+            loop(slots // 2, give_first_sums)
+            wait_sides_sent(0, 0)
+        else:
+            loop(slots - 1, give_sides)
+            make_gates(1)
             loop(tiles, lambda t: wait_sums_sent(0, t))
-        loop(slots, give_sums)
-        if layer == 0:
-            wait_sides_sent(0, 0)
+            loop(slots, give_sums)
         loop(tiles, take_sums)
 
+    loop(slots, lambda slot: wait_twin(slot, twin_sent))
     loop(slots, lambda slot: wait_sides_sent(1, slot))
     loop(tiles, lambda t: wait_sums_sent(1, t))
 
@@ -294,7 +430,9 @@
                 pltpu.SemaphoreType.DMA((tiles,)),
                 pltpu.SemaphoreType.DMA((len(operands) - 1,)),
                 pltpu.VMEM((slots, n, 2, rows, cols), BF16),
-                pltpu.VMEM((2, slots, 2, cols, cols), BF16),
+                pltpu.VMEM((slots, cols, cols), BF16),
+                pltpu.VMEM((slots, 2, cols, cols), BF16),
+                pltpu.VMEM((slots, 2, cols, cols), BF16),
                 pltpu.VMEM((tiles, slots, cols, LANES), F32),
                 pltpu.VMEM((tiles, channels * pitch, LANES), F32),
                 pltpu.VMEM((tiles, n * pitch, LANES), F32),
@@ -313,6 +451,8 @@
                 pltpu.SemaphoreType.DMA((2, slots)),
                 pltpu.SemaphoreType.DMA((2, tiles)),
                 pltpu.SemaphoreType.DMA((2, tiles)),
+                pltpu.SemaphoreType.DMA((slots,)),
+                pltpu.SemaphoreType.DMA((slots,)),
             ],
             compiler_params=pltpu.CompilerParams(collective_id=0, has_side_effects=True, vmem_limit_bytes=54 * 2 ** 20),
             name="triangle_pair",

time: 195 us -> 191 us (0.979)
  Pallas kernels: 193 us -> 189 us
    pallas_call x1, Pallas kernels: 193 us -> 189 us  [local_layers(): pl.pallas_call(functools.partial(kernel, n, side, slots, pitch), out_shap...]
where the time goes in v5:
time: 191 us; the launch traced here: 190 us
  Pallas kernels  189 us (99%)
    pallas_call x1, Pallas kernels, local_layers(): pl.pallas_call(functools.partial(kernel, n, side, slots, pitch), out_shap...  189 us

profile of v5, /device:TPU:97, one launch (start us, length us, event | category | flops | bytes accessed | tf_op | source)
XLA Modules:
  0.0 190.5 jit_solution(4598793166872836999)
XLA Ops:
  0.0 189.1 %triangle_pair.1 = bf16[16,512,128]{2,1,0:T(8,128)(2,1)S(1)} custom-call(bf16[16,512,128]{2,1,0:T(8,128)(2,1)} %z_hbm.1, s32[16,512]{1,0:T(8,128)} %mask_hbm.1, bf16[2,2,128]{2,1,0:T(2,128)(2,1)} %ln_in_hbm.1, bf16[2,128,512]{2,1,0:T(8,128)(2,1)} %w_proj_hbm.1, bf16[2,512]{1,0:T(2,128)(2,1)} %b_proj_hbm.1, bf16[2,128,128]{2,1,0:T(8,128)(2,1)} %w_gate_hbm.1, ...), custom_call_target="tpu_custom_call" | custom-call | tf_op jit(solution)/shard_map/triangle_pair/pallas_call | solution.py:424
  189.1 1.3 copy.12

commit v6 on v5

--- a/solution.py
+++ b/solution.py
@@ -52,7 +52,7 @@
            wp, bp, wg, wo, vec, keep, sides_sent, sides_here, sums_sent, sums_here, twin_sent, twin_here):
     rows, cols, channels = z_ref.shape
     tiles = cols // LANES
-    group = 4
+    group = 16
     order = send_order(side)
     me = lax.axis_index("dap")
     core, place = lax.rem(me, 2), me // 2
@@ -267,15 +267,15 @@
         loop(n // unroll, some)
 
     def make_sides(layer, slot):
-        loop(rows, lambda i: gated(layer, slot, [(i, t) for t in range(tiles)]))
-        pack(slot, range(tiles), 1)
+        loop(rows // 2, lambda step: gated(layer, slot, [(2 * step + k, t) for k in range(2) for t in range(tiles)]))
+        pack(slot, range(tiles), 2)
 
     def make_sides_part(layer, slot, t):
         loop(rows // group, lambda step: gated(layer, slot, [(step * group + k, t) for k in range(group)]))
-        pack(slot, [t], 4)
+        pack(slot, [t], 8)
 
     def make_sides_half(layer, slot, t):
-        loop(rows // 2, lambda step: gated(layer, slot, [(2 * step + k, t + j) for k in range(2) for j in range(2)]))
+        loop(rows // 4, lambda step: gated(layer, slot, [(4 * step + k, t + j) for k in range(4) for j in range(2)]))
         pack(slot, [t, t + 1], 2)
 
     def make_gates(layer):

time: 191 us -> 186 us (0.974)
  Pallas kernels: 189 us -> 185 us
    pallas_call x1, Pallas kernels: 189 us -> 185 us  [local_layers(): pl.pallas_call(functools.partial(kernel, n, side, slots, pitch), out_shap...]
where the time goes in v6:
time: 186 us
  Pallas kernels  185 us (99%)
    pallas_call x1, Pallas kernels, local_layers(): pl.pallas_call(functools.partial(kernel, n, side, slots, pitch), out_shap...  185 us

profile of v6, /device:TPU:97, one launch (start us, length us, event | category | flops | bytes accessed | tf_op | source)
XLA Modules:
  0.0 186.0 jit_solution(14275733534612527538)
XLA Ops:
  0.0 184.7 %triangle_pair.1 = bf16[16,512,128]{2,1,0:T(8,128)(2,1)S(1)} custom-call(bf16[16,512,128]{2,1,0:T(8,128)(2,1)} %z_hbm.1, s32[16,512]{1,0:T(8,128)} %mask_hbm.1, bf16[2,2,128]{2,1,0:T(2,128)(2,1)} %ln_in_hbm.1, bf16[2,128,512]{2,1,0:T(8,128)(2,1)} %w_proj_hbm.1, bf16[2,512]{1,0:T(2,128)(2,1)} %b_proj_hbm.1, bf16[2,128,128]{2,1,0:T(8,128)(2,1)} %w_gate_hbm.1, ...), custom_call_target="tpu_custom_call" | custom-call | tf_op jit(solution)/shard_map/triangle_pair/pallas_call | solution.py:424
  184.7 1.3 copy.12

commit v7 on v6

--- a/solution.py
+++ b/solution.py
@@ -16,8 +16,8 @@
 
 
 def send_order(side):
-    near = [(1, 0), (-1, 0), (0, 1), (0, -1), (2, 0), (0, 2), (1, 1), (-1, -1), (1, -1), (-1, 1), (2, 2), (1, 2),
-            (-1, 2), (2, 1), (2, -1), (0, 0)]
+    near = [(2, 2), (1, 0), (-1, 2), (0, -1), (2, 1), (-1, 0), (1, -1), (0, 2), (1, 2), (-1, -1), (2, 0), (0, 1),
+            (1, 1), (2, -1), (-1, 1), (0, 0)]
     found, order = set(), []
     for dc in range(2):
         for dx, dy in near + [(x, y) for x in range(side) for y in range(side)]:

time: 186 us -> 186 us (level)
  no operation moved by 1% of the time
where the time goes in v7:
time: 186 us
  Pallas kernels  184 us (99%)
    pallas_call x1, Pallas kernels, local_layers(): pl.pallas_call(functools.partial(kernel, n, side, slots, pitch), out_shap...  184 us

profile of v7, /device:TPU:97, one launch (start us, length us, event | category | flops | bytes accessed | tf_op | source)
XLA Modules:
  0.0 185.5 jit_solution(7048225240831568145)
XLA Ops:
  0.0 184.2 %triangle_pair.1 = bf16[16,512,128]{2,1,0:T(8,128)(2,1)S(1)} custom-call(bf16[16,512,128]{2,1,0:T(8,128)(2,1)} %z_hbm.1, s32[16,512]{1,0:T(8,128)} %mask_hbm.1, bf16[2,2,128]{2,1,0:T(2,128)(2,1)} %ln_in_hbm.1, bf16[2,128,512]{2,1,0:T(8,128)(2,1)} %w_proj_hbm.1, bf16[2,512]{1,0:T(2,128)(2,1)} %b_proj_hbm.1, bf16[2,128,128]{2,1,0:T(8,128)(2,1)} %w_gate_hbm.1, ...), custom_call_target="tpu_custom_call" | custom-call | tf_op jit(solution)/shard_map/triangle_pair/pallas_call | solution.py:424
  184.2 1.3 copy.12
